TPU v7x, 256 devices: a whole 4x4x8 slice. The times are simulated.
256 devices in a mesh: dp: 4 (over x), vocab: 64 (over z, y, core).
Axes of the slice: x: 4, y: 4, z: 8, core: 2. Of those that a mesh axis runs over, the one named last changes fastest.
Arguments:
- prefill_hidden: bfloat16 [1024, 7168], P(('dp', 'vocab')), may hold values from -60 to 60
- decode_hidden: bfloat16 [256, 7168], P(('dp', 'vocab')), may hold values from -60 to 60
- lm_head: bfloat16 [7168, 129280], P('dp', 'vocab'), as said below
- prefill_targets: int32 [1024], P(('dp', 'vocab')), may hold values from 0 to 129279
- decode_targets: int32 [256], P(('dp', 'vocab')), may hold values from 0 to 129279
- decode_live: int32 [4], P('dp'), may hold values from 1 to 64
Outputs:
- prefill_logprob: float32 [1024], P(('dp', 'vocab'))
- decode_logprob: float32 [256], P(('dp', 'vocab'))
Inputs may be any that keep to these rules, and one draw needn't show every extreme that they name: `lm_head`: entries of order one over the square root of 7168.
All inputs are finite; a program needn't handle non-finite values.
Results may differ from a plain program's by a relative error of at most 0.0003.
Values may be sent and summed in bfloat16 or wider, within the bound.
A program may use at most 128 MiB of HBM per device.

v0:
```python
import jax
import jax.numpy as jnp
from jax import lax
from jax.sharding import Mesh
from jax.sharding import PartitionSpec as P

VOCAB = ("vocab_0", "vocab_1", "vocab_2")
DP_VOCAB = ("dp", "vocab_0", "vocab_1", "vocab_2")


def gathered_once(value, axis):
    leaves = jax.tree.leaves(value)
    sequence = sorted(range(len(leaves)), key=lambda k: -leaves[k].size)
    width = (1, *leaves[sequence[0]].shape)[-1]
    lines = [
        jnp.pad(leaves[k].reshape(-1), (0, -leaves[k].size % width)).reshape(-1, width)
        for k in sequence
    ]
    both, at, found = (lax.all_gather(jnp.concatenate(lines), axis), 0, {})
    for k, line in zip(sequence, lines):
        slab = both[:, at : at + len(line)].reshape(len(both), -1)
        found[k] = slab[:, : leaves[k].size].reshape(-1, *leaves[k].shape)
        at += len(line)
    numbers = iter(range(len(leaves)))
    return jax.tree.map(lambda _: found[next(numbers)], value)


def joined_all(value, axes, combine):
    for axis in axes:
        pieces = gathered_once(value, axis)
        value = jax.tree.map(lambda part: part[0], pieces)
        for k in range(1, lax.axis_size(axis)):
            value = combine(value, jax.tree.map(lambda part: part[k], pieces))
    return value


def softmax_join(left, right):
    new_top = jnp.maximum(left[0], right[0])
    totals = left[1] * jnp.exp(left[0] - new_top) + right[1] * jnp.exp(right[0] - new_top)
    return (new_top, totals, left[2] + right[2])


def body(prefill_hidden, decode_hidden, lm_head, prefill_targets, decode_targets, decode_live):
    pre_rows = prefill_hidden.shape[0]
    dec_rows = decode_hidden.shape[0]
    own_count = pre_rows + dec_rows
    hidden = jnp.concatenate([prefill_hidden, decode_hidden], axis=0)
    targets = jnp.concatenate([prefill_targets, decode_targets], axis=0)
    shard_vocab = lm_head.shape[1]
    vocab_offset = lax.axis_index(VOCAB) * shard_vocab
    group_hidden, group_targets = (
        lax.all_gather(hidden, VOCAB, axis=0, tiled=True),
        lax.all_gather(targets, VOCAB, axis=0, tiled=True),
    )
    every_rows = lax.all_to_all(group_hidden, "dp", split_axis=1, concat_axis=0, tiled=True)
    logits = lax.psum_scatter(
        jnp.dot(every_rows, lm_head, preferred_element_type=jnp.float32),
        "dp",
        scatter_dimension=0,
        tiled=True,
    )
    local_top = jnp.max(logits, axis=1)
    target_hit = (group_targets - vocab_offset)[:, None] == jnp.arange(
        shard_vocab, dtype=jnp.int32
    )[None, :]
    local_picked = jnp.sum(jnp.where(target_hit, logits, jnp.float32(0.0)), axis=1)
    own_start = lax.axis_index(VOCAB) * own_count
    local_total = jnp.sum(jnp.exp(logits - local_top[:, None]), axis=1)
    row_top, totals, picked = joined_all(
        (local_top, local_total, local_picked), VOCAB, softmax_join
    )
    group_values = picked - (row_top + jnp.log(totals))
    own_values = lax.dynamic_slice_in_dim(group_values, own_start, own_count, 0)
    prefill_logprob = own_values[:pre_rows]
    positions = lax.axis_index(VOCAB) * dec_rows + jnp.arange(dec_rows, dtype=jnp.int32)
    decode_logprob = jnp.where(positions < decode_live[0], own_values[pre_rows:], jnp.float32(0.0))
    return (prefill_logprob, decode_logprob)


def solution(mesh):
    split = Mesh(
        mesh.devices.reshape(mesh.shape["dp"], 8, 4, 2), ("dp", "vocab_0", "vocab_1", "vocab_2")
    )
    placed = (
        P(DP_VOCAB, None),
        P(DP_VOCAB, None),
        P("dp", VOCAB),
        P(DP_VOCAB),
        P(DP_VOCAB),
        P("dp"),
    )
    return jax.shard_map(
        body, mesh=split, in_specs=placed, out_specs=(P(DP_VOCAB), P(DP_VOCAB)), check_vma=False
    )
```

profile of v0, /device:TPU:1, one launch (start us, length us, event | category | flops | bytes accessed | tf_op | source)
XLA Modules:
  0.0 330.9 jit_solution(16008943737655418088)
XLA Ops:
  7.2 0.0 all-gather.9.cloned.1.call-start
  7.2 1.5 maximum_bitcast_fusion
  8.8 0.0 all-gather.9.cloned.1.call-update
  8.8 0.0 reduce-scatter.2.cloned.1.call-start
  8.8 87.9 %all-gather.9.cloned.1.call-done = bf16[64,5,7168]{2,1,0:T(8,128)(2,1)} async-done(((bf16[1,5,7168]{2,1,0:T(8,128)(2,1)}), bf16[64,5,7168]{2,1,0:T(8,128)(2,1)}) %all-gather.9.cloned.1.call-update) | async-done | bytes 4587536 | tf_op jit(solution)/shard_map/all_gather | solution.py:52
  96.7 11.4 %all_to_all.14 = bf16[320,4,1792]{2,1,0:T(4,128)(2,1)} reshape(bf16[64,5,7168]{2,1,0:T(8,128)(2,1)} %all-gather.9.cloned.1.call-done) | data formatting | bytes 9175040 | tf_op jit(solution)/shard_map/all_to_all | solution.py:55
  108.1 0.0 slice-start
  108.1 3.0 copy.9
  111.1 0.0 slice-start.1
  111.2 56.6 %all_to_all.19 = bf16[320,4,1792]{2,0,1:T(8,128)(2,1)S(1)} all-to-all(bf16[320,4,1792]{2,0,1:T(8,128)(2,1)S(1)} %copy.9), channel_id=1, replica_groups=mesh['dp'=4,'vocab_0'=8,'vocab_1'=4,'vocab_2'=2] {'dp'}, dimensions={1} | all-to-all | bytes 9175040 | tf_op jit(solution)/shard_map/all_to_all | solution.py:55
  167.8 0.0 slice-done
  167.8 0.0 slice-done.1
  167.8 12.4 %fusion.47 = f32[1280,2020]{1,0:T(8,128)} fusion(bf16[1280,1792]{1,0:T(8,128)(2,1)S(1)} %bitcast.248, bf16[1792,2020]{0,1:T(8,128)(2,1)S(1)} %bitcast.250), kind=kOutput, calls=%fused_computation.95 | convolution fusion | flops 9266790400 | bytes 22169600 | tf_op jit(solution)/shard_map/dot_general | solution.py:57
  180.2 0.0 copy-start.1
  180.2 0.0 copy-start
  180.2 0.0 reduce-scatter.2.cloned.1.call-update
  181.5 0.0 copy-done.1
  181.5 0.6 dynamic-slice
  182.8 0.0 copy-done
  182.8 0.2 add_dynamic-update-slice_fusion
  183.0 15.0 %all-reduce = s32[320]{0:T(512)S(1)} all-reduce(s32[320]{0:T(512)S(1)} %add_dynamic-update-slice_fusion), channel_id=1, replica_groups=mesh['dp'=4,'vocab_0'=8,'vocab_1'=4,'vocab_2'=2] {'vocab_0','vocab_1','v..., use_global_device_ids=true, to_apply=%add | all-reduce | flops 320 | bytes 2560
  198.0 78.1 %reduce-scatter.2.cloned.1.call-done = f32[320,2020]{1,0:T(8,128)} async-done(((f32[1280,2020]{1,0:T(8,128)}), f32[320,2020]{1,0:T(8,128)}) %reduce-scatter.2.cloned.1.call-update) | async-done | bytes 2585616 | tf_op jit(solution)/shard_map/reduce_scatter | solution.py:56
  276.1 2.0 reduce_max.9
  278.0 2.5 exponential_reduce_fusion
  280.6 20.2 %all-gather.4 = f32[8,3,320]{2,1,0:T(4,128)S(1)} all-gather(f32[1,3,320]{2,1,0:T(4,128)S(1)} %maximum_bitcast_fusion.1), channel_id=2, replica_groups=mesh['dp'=4,'vocab_0'=8,'vocab_1'=4,'vocab_2'=2] {'vocab_0'}, dimensions={0}, use_global_device_ids=true | all-gather | bytes 34560 | tf_op jit(solution)/shard_map/all_gather | solution.py:19
  300.9 9.4 %all-gather.5 = f32[4,3,320]{2,1,0:T(4,128)S(1)} all-gather(f32[1,3,320]{2,1,0:T(4,128)S(1)} %maximum_bitcast_fusion.2), channel_id=3, replica_groups=mesh['dp'=4,'vocab_0'=8,'vocab_1'=4,'vocab_2'=2] {'vocab_1'}, dimensions={0}, use_global_device_ids=true | all-gather | bytes 19200 | tf_op jit(solution)/shard_map/all_gather | solution.py:19
  310.4 11.2 %all-gather.6 = f32[2,3,320]{2,1,0:T(4,128)S(1)} all-gather(f32[1,3,320]{2,1,0:T(4,128)S(1)} %maximum_bitcast_fusion.3), channel_id=4, replica_groups=mesh['dp'=4,'vocab_0'=8,'vocab_1'=4,'vocab_2'=2] {'vocab_2'}, dimensions={0}, use_global_device_ids=true | all-gather | bytes 11520 | tf_op jit(solution)/shard_map/all_gather | solution.py:19
  321.6 0.1 dynamic_slice.3
  321.7 0.0 copy-start.2
  321.7 0.6 slice.268
  322.9 0.0 copy-done.2
  (15 shorter events, 0.2 us)
Async XLA Ops:
  7.2 89.5 %all-gather.9.cloned.1.call-start = ((), (), s32[]{:S(2)}) async-start(), calls=%async_computation.3 | async-start | bytes 7454720 | tf_op jit(solution)/shard_map/all_gather | solution.py:52
  8.8 267.3 %reduce-scatter.2.cloned.1.call-start = ((), (), s32[]{:S(2)}) async-start(), calls=%async_computation.2 | async-start | bytes 13107200 | tf_op jit(solution)/shard_map/reduce_scatter | solution.py:56
  108.1 59.6 %slice-start = ((s8[7254016]{0:T(1024)(128)(4,1)}), s8[4194304]{0:T(1024)(128)(4,1)S(1)}, s32[]{:S(2)}) async-start(s8[7254016]{0:T(1024)(128)(4,1)} %bitcast.249), calls=%async_computation.4 | async-start | bytes 8388608
  111.1 56.6 %slice-start.1 = ((s8[7254016]{0:T(1024)(128)(4,1)}), s8[3059712]{0:T(1024)(128)(4,1)S(1)}, s32[]{:S(2)}) async-start(s8[7254016]{0:T(1024)(128)(4,1)} %bitcast.249), calls=%async_computation.5 | async-start | bytes 6119424
  180.2 1.3 copy-start.1
  180.2 2.6 copy-start
  321.7 1.2 copy-start.2
Sparse Core Ops, SparseCore 0:
  10.7 85.9 all-gather.8
  180.3 95.6 reduce-scatter.1
where the time goes:
time: 331 us
  waiting for transfers between devices  166 us (50%)
  blocking collectives  112 us (34%)
  between operations  17.9 us (5%)
  local copies, waits for them, and re-layouts  15.7 us (5%)
  matrix products  12.4 us (4%)
  other arithmetic  6.4 us (2%)
    all_gather x1, waiting for transfers between devices, body(): lax.all_gather(hidden, VOCAB, axis=0, tiled=True)  87.9 us
    reduce_scatter x1, waiting for transfers between devices, body(): lax.psum_scatter(jnp.dot(every_rows, lm_head, preferred_element_type=jnp....  78.1 us
    all_to_all x1, blocking collectives, body(): lax.all_to_all(group_hidden, 'dp', split_axis=1, concat_axis=0, tiled=True)  56.6 us
    all_gather x3, blocking collectives, gathered_once(): both, at, found = (lax.all_gather(jnp.concatenate(lines), axis), 0, {})  40.8 us
    unnamed x1, blocking collectives  15 us
    all_to_all x2, local copies, waits for them, and re-layouts, body(): lax.all_to_all(group_hidden, 'dp', split_axis=1, concat_axis=0, tiled=True)  14.5 us
    dot_general x1, matrix products, body(): jnp.dot(every_rows, lm_head, preferred_element_type=jnp.float32)  12.4 us
  transfers between devices with their start and end apart: 2, of which 2 were waited for; matrix products, arithmetic and copies ran while one was open for 0% of the time, Pallas kernels for 0%

commit v1 on v0

--- a/solution.py
+++ b/solution.py
@@ -49,7 +49,9 @@
     shard_vocab = lm_head.shape[1]
     vocab_offset = lax.axis_index(VOCAB) * shard_vocab
     group_hidden, group_targets = (
-        lax.all_gather(hidden, VOCAB, axis=0, tiled=True),
+        jnp.concatenate(
+            lax.all_to_all(jnp.stack([hidden] * lax.axis_size(VOCAB)), VOCAB, 0, 0), axis=0
+        ),
         lax.all_gather(targets, VOCAB, axis=0, tiled=True),
     )
     every_rows = lax.all_to_all(group_hidden, "dp", split_axis=1, concat_axis=0, tiled=True)

time: 331 us -> 420 us (1.27)
  blocking collectives: 112 us -> 289 us
  waiting for transfers between devices: 166 us -> 77.6 us
    all_to_all x0 -> x1, blocking collectives: none -> 176 us  [body(): lax.all_to_all(jnp.stack([hidden] * lax.axis_size(VOCAB)), VOCAB, 0, 0)]
    all_gather x1 -> x0, waiting for transfers between devices: 87.9 us -> none  [body(): lax.all_gather(hidden, VOCAB, axis=0, tiled=True)]
  transfers between devices with their start and end apart: 2 -> 1, of which waited for: 2 -> 1; matrix products, arithmetic and copies ran while one was open for 0% -> 0% of each run, Pallas kernels for 0% -> 0%
where the time goes in v1:
time: 420 us; the launch traced here: 419 us
  blocking collectives  289 us (69%)
  waiting for transfers between devices  77.6 us (18%)
  between operations  17.9 us (4%)
  local copies, waits for them, and re-layouts  16.6 us (4%)
  matrix products  12.4 us (3%)
  other arithmetic  5.75 us (1%)
    all_to_all x1, blocking collectives, body(): lax.all_to_all(jnp.stack([hidden] * lax.axis_size(VOCAB)), VOCAB, 0, 0)  176 us
    reduce_scatter x1, waiting for transfers between devices, body(): lax.psum_scatter(jnp.dot(every_rows, lm_head, preferred_element_type=jnp....  77.6 us
    all_to_all x1, blocking collectives, body(): lax.all_to_all(group_hidden, 'dp', split_axis=1, concat_axis=0, tiled=True)  55.5 us
    all_gather x3, blocking collectives, gathered_once(): both, at, found = (lax.all_gather(jnp.concatenate(lines), axis), 0, {})  40.8 us
    unnamed x1, blocking collectives  16.5 us
    all_to_all x2, local copies, waits for them, and re-layouts, body(): lax.all_to_all(group_hidden, 'dp', split_axis=1, concat_axis=0, tiled=True)  14.5 us
    dot_general x1, matrix products, body(): jnp.dot(every_rows, lm_head, preferred_element_type=jnp.float32)  12.4 us
  transfers between devices with their start and end apart: 1, of which 1 were waited for; matrix products, arithmetic and copies ran while one was open for 0% of the time, Pallas kernels for 0%

profile of v1, /device:TPU:1, one launch (start us, length us, event | category | flops | bytes accessed | tf_op | source)
XLA Modules:
  0.0 419.2 jit_solution(12714442648289137944)
XLA Ops:
  7.2 0.0 reduce-scatter.2.cloned.1.call-start
  7.2 0.9 pad_maximum_fusion
  8.1 0.9 stack.2
  9.0 176.1 %all_to_all.24 = bf16[64,5,7168]{2,1,0:T(8,128)(2,1)} all-to-all(bf16[64,5,7168]{2,1,0:T(8,128)(2,1)S(1)} %stack.2), channel_id=1, replica_groups=mesh['dp'=4,'vocab_0'=8,'vocab_1'=4,'vocab_2'=2] {'vocab_0','vocab_1','v..., dimensions={0} | all-to-all | bytes 9175040 | tf_op jit(solution)/shard_map/all_to_all | solution.py:53
  185.1 11.4 %all_to_all.18 = bf16[320,4,1792]{2,1,0:T(4,128)(2,1)} reshape(bf16[64,5,7168]{2,1,0:T(8,128)(2,1)} %all_to_all.24) | data formatting | bytes 9175040 | tf_op jit(solution)/shard_map/all_to_all | solution.py:57
  196.5 0.0 slice-start
  196.5 3.0 copy.9
  199.5 0.0 slice-start.1
  199.6 55.5 %all_to_all.25 = bf16[320,4,1792]{2,0,1:T(8,128)(2,1)S(1)} all-to-all(bf16[320,4,1792]{2,0,1:T(8,128)(2,1)S(1)} %copy.9), channel_id=1, replica_groups=mesh['dp'=4,'vocab_0'=8,'vocab_1'=4,'vocab_2'=2] {'dp'}, dimensions={1} | all-to-all | bytes 9175040 | tf_op jit(solution)/shard_map/all_to_all | solution.py:57
  255.1 0.0 slice-done
  255.1 0.0 slice-done.1
  255.1 12.4 %fusion.47 = f32[1280,2020]{1,0:T(8,128)} fusion(bf16[1280,1792]{1,0:T(8,128)(2,1)S(1)} %bitcast.246, bf16[1792,2020]{0,1:T(8,128)(2,1)S(1)} %bitcast.248), kind=kOutput, calls=%fused_computation.95 | convolution fusion | flops 9266790400 | bytes 22169600 | tf_op jit(solution)/shard_map/dot_general | solution.py:59
  267.5 0.0 copy-start.1
  267.5 0.0 copy-start
  267.5 0.0 reduce-scatter.2.cloned.1.call-update
  268.8 0.0 copy-done.1
  268.9 0.6 dynamic-slice
  270.1 0.0 copy-done
  270.1 0.2 add_dynamic-update-slice_fusion
  270.3 16.5 %all-reduce = s32[320]{0:T(512)S(1)} all-reduce(s32[320]{0:T(512)S(1)} %add_dynamic-update-slice_fusion), channel_id=1, replica_groups=mesh['dp'=4,'vocab_0'=8,'vocab_1'=4,'vocab_2'=2] {'vocab_0','vocab_1','v..., use_global_device_ids=true, to_apply=%add | all-reduce | flops 320 | bytes 2560
  286.8 77.6 %reduce-scatter.2.cloned.1.call-done = f32[320,2020]{1,0:T(8,128)} async-done(((f32[1280,2020]{1,0:T(8,128)}), f32[320,2020]{1,0:T(8,128)}) %reduce-scatter.2.cloned.1.call-update) | async-done | bytes 2585616 | tf_op jit(solution)/shard_map/reduce_scatter | solution.py:58
  364.4 2.0 reduce_max.9
  366.4 2.5 exponential_reduce_fusion
  368.9 20.2 %all-gather.3 = f32[8,3,320]{2,1,0:T(4,128)S(1)} all-gather(f32[1,3,320]{2,1,0:T(4,128)S(1)} %maximum_bitcast_fusion), channel_id=2, replica_groups=mesh['dp'=4,'vocab_0'=8,'vocab_1'=4,'vocab_2'=2] {'vocab_0'}, dimensions={0}, use_global_device_ids=true | all-gather | bytes 34560 | tf_op jit(solution)/shard_map/all_gather | solution.py:19
  389.2 9.4 %all-gather.4 = f32[4,3,320]{2,1,0:T(4,128)S(1)} all-gather(f32[1,3,320]{2,1,0:T(4,128)S(1)} %maximum_bitcast_fusion.1), channel_id=3, replica_groups=mesh['dp'=4,'vocab_0'=8,'vocab_1'=4,'vocab_2'=2] {'vocab_1'}, dimensions={0}, use_global_device_ids=true | all-gather | bytes 19200 | tf_op jit(solution)/shard_map/all_gather | solution.py:19
  398.7 11.2 %all-gather.5 = f32[2,3,320]{2,1,0:T(4,128)S(1)} all-gather(f32[1,3,320]{2,1,0:T(4,128)S(1)} %maximum_bitcast_fusion.2), channel_id=4, replica_groups=mesh['dp'=4,'vocab_0'=8,'vocab_1'=4,'vocab_2'=2] {'vocab_2'}, dimensions={0}, use_global_device_ids=true | all-gather | bytes 11520 | tf_op jit(solution)/shard_map/all_gather | solution.py:19
  409.9 0.1 dynamic_slice.3
  410.0 0.0 copy-start.2
  410.0 0.6 slice.268
  411.2 0.0 copy-done.2
  (15 shorter events, 0.2 us)
Async XLA Ops:
  7.2 357.2 %reduce-scatter.2.cloned.1.call-start = ((), (), s32[]{:S(2)}) async-start(), calls=%async_computation.3 | async-start | bytes 13107200 | tf_op jit(solution)/shard_map/reduce_scatter | solution.py:58
  196.5 58.6 %slice-start = ((s8[7254016]{0:T(1024)(128)(4,1)}), s8[4194304]{0:T(1024)(128)(4,1)S(1)}, s32[]{:S(2)}) async-start(s8[7254016]{0:T(1024)(128)(4,1)} %bitcast.247), calls=%async_computation.4 | async-start | bytes 8388608
  199.5 55.5 %slice-start.1 = ((s8[7254016]{0:T(1024)(128)(4,1)}), s8[3059712]{0:T(1024)(128)(4,1)S(1)}, s32[]{:S(2)}) async-start(s8[7254016]{0:T(1024)(128)(4,1)} %bitcast.247), calls=%async_computation.5 | async-start | bytes 6119424
  267.5 1.3 copy-start.1
  267.5 2.6 copy-start
  410.0 1.2 copy-start.2
Sparse Core Ops, SparseCore 0:
  267.7 96.6 reduce-scatter.1
